TPU v7x, 256 devices: a whole 4x4x8 slice. The times are simulated.
256 devices in a mesh: replica: 16 (over x_lo, z), expert: 16 (over x_hi, y, core).
Axes of the slice: x: 4 (x_hi: 2, x_lo: 2; x = x_hi * 2 + x_lo), y: 4, z: 8, core: 2. Of those that a mesh axis runs over, the one named last changes fastest.
Arguments:
- weights: bfloat16 [16, 2048, 512], P('expert'), may hold values from -3 to 3
- momentum: float32 [16, 16, 2048, 512], P('replica', 'expert'), may hold values from -6 to 6
- gradients: bfloat16 [2, 16, 16, 2048, 512], P(None, 'replica', 'expert'), may hold values from -6 to 6
- outer_momentum: float32 [16, 2048, 512], P('expert', 'replica'), may hold values from -2 to 2
Outputs:
- new_weights: bfloat16 [16, 2048, 512], P('expert')
- new_outer: float32 [16, 2048, 512], P('expert', 'replica')
All inputs are finite; a program needn't handle non-finite values.
Results may differ from a plain program's by a relative error of at most 0.0075.
Values may be sent and summed in bfloat16 or wider, within the bound.
A program may use at most 64 MiB of HBM per device.

v0:
```python
import math

import jax
import jax.numpy as jnp
from jax import lax
from jax.sharding import Mesh
from jax.sharding import PartitionSpec as P

ROWS = 2048
STEPS = 2
NS_ITERS = 3
REPLICA = ("replica_0", "replica_1")


coef_a = 3.4445
coef_b = -4.775
coef_c = 2.0315
inner_beta = 0.9
outer_beta = 0.9
outer_rate = 1.0
epsilon = 1e-07


def partner_2(block, axis, stride):
    count = lax.axis_size(axis)
    route = []
    for low in range(count):
        high = low | 1 << stride
        if high != low and high < count:
            route += [(low, high), (high, low)]
    return lax.ppermute(block, axis, route)


def reduced_to_own(pieces, axes, sequence):
    shape = [lax.axis_size(a) for a in axes]
    pieces = pieces.reshape(*shape, *pieces.shape[1:])
    pieces = pieces.transpose(*sequence, *range(len(axes), pieces.ndim))
    pieces = pieces.reshape(-1, *pieces.shape[len(axes) :])
    for k in sequence:
        pieces = lax.psum_scatter(pieces, axes[k], scatter_dimension=0, tiled=True)
    return pieces[0]


def in_blocks(x, dim, devices):
    before, after = (x.shape[:dim], x.shape[dim + 1 :])
    return jnp.moveaxis(x.reshape(*before, devices, -1, *after), dim, 0)


def summed_rows(x, axes, sequence, dim):
    devices = lax.axis_size(axes)
    return reduced_to_own(in_blocks(x, dim, devices), axes, sequence)


def in_order(pieces, dim):
    shape = list(pieces.shape[1:])
    shape[dim] *= pieces.shape[0]
    return jnp.moveaxis(pieces, 0, dim).reshape(shape)


def copy_for_each(x, axis):
    devices = lax.axis_size(axis)
    return lax.all_to_all(jnp.broadcast_to(x[None], (devices, *x.shape)), axis, 0, 0, tiled=True)


def gather_directly(x, axis, dim):
    return in_order(copy_for_each(x, axis), dim)


def orthogonal(matrix):
    norm_value = jnp.sqrt(jnp.sum(matrix * matrix, axis=(1, 2), keepdims=True))
    current = (matrix / (norm_value + epsilon)).astype(jnp.bfloat16)
    for index in range(NS_ITERS):
        gram = jnp.einsum(
            "erc,erd->ecd", current, current, preferred_element_type=jnp.float32
        ).astype(jnp.bfloat16)
        square = jnp.einsum("ecd,edf->ecf", gram, gram, preferred_element_type=jnp.float32)
        poly = (coef_b * gram.astype(jnp.float32) + coef_c * square).astype(jnp.bfloat16)
        product = jnp.einsum("erc,ecd->erd", current, poly, preferred_element_type=jnp.float32)
        current = (coef_a * current.astype(jnp.float32) + product).astype(jnp.bfloat16)
    return current


def per_device(weights, momentum, gradients, outer_momentum):
    update_scale = 0.5 * 0.2 * math.sqrt(ROWS)
    replicas = lax.axis_size(REPLICA)
    moment = momentum[0]
    local = weights
    for step in range(STEPS):
        moment = inner_beta * moment + gradients[step, 0].astype(jnp.float32)
        partner = partner_2(moment.astype(jnp.bfloat16), REPLICA, step).astype(moment.dtype)
        moment = 0.5 * (moment + partner)
        ortho = orthogonal(moment)
        local = (local.astype(jnp.float32) - update_scale * ortho.astype(jnp.float32)).astype(
            jnp.bfloat16
        )
    change = weights.astype(jnp.float32) - local.astype(jnp.float32)
    share = outer_momentum.shape[1]
    first_row = lax.axis_index(REPLICA) * share
    total = summed_rows(change.astype(jnp.bfloat16), REPLICA, (1, 0), 1).astype(jnp.float32)
    fresh = outer_beta * outer_momentum + total / replicas
    own_rows = lax.dynamic_slice_in_dim(weights, first_row, share, 1).astype(jnp.float32)
    rows_new = (own_rows - outer_rate * fresh).astype(jnp.bfloat16)
    result = gather_directly(rows_new, REPLICA, 1)
    return (result, fresh)


def solution(mesh):
    split = Mesh(
        mesh.devices.reshape(2, 8, mesh.shape["expert"]), ("replica_0", "replica_1", "expert")
    )
    return jax.shard_map(
        per_device,
        mesh=split,
        in_specs=(
            P("expert", None, None),
            P(REPLICA, "expert", None, None),
            P(None, REPLICA, "expert", None, None),
            P("expert", REPLICA, None),
        ),
        out_specs=(P("expert", None, None), P("expert", REPLICA, None)),
        check_vma=False,
    )
```

profile of v0, /device:TPU:10, one launch (start us, length us, event | category | flops | bytes accessed | tf_op | source)
XLA Modules:
  0.0 331.1 jit_solution(13834265316615700483)
XLA Ops:
  7.2 0.0 reduce-scatter.3.cloned.1.call-start
  7.2 0.0 copy-start.1
  7.2 0.0 copy-start.2
  7.2 3.8 %fusion.8 = bf16[1,2048,512]{2,1,0:T(8,128)(2,1)S(1)} fusion(f32[1,1,2048,512]{3,2,1,0:T(8,128)} %param.5, bf16[2,1,1,2048,512]{4,3,2,1,0:T(8,128)(2,1)} %param.6), kind=kLoop, calls=%fused_computation.25 | loop fusion | flops 4194304 | bytes 8388608 | tf_op jit(solution)/shard_map/convert_element_type | solution.py:90
  11.0 2.0 collective-permute-start
  13.0 45.6 %collective-permute-done = bf16[1,2048,512]{2,1,0:T(8,128)(2,1)S(1)} collective-permute-done((bf16[1,2048,512]{2,1,0:T(8,128)(2,1)S(1)}, bf16[1,2048,512]{2,1,0:T(8,128)(2,1)S(1)}, u32[]{:S(2)}, u32[]{:S(2)}) %collective-permute-start) | collective-permute-done | bytes 2097184 | tf_op jit(solution)/shard_map/ppermute | solution.py:31
  58.6 0.0 copy-done.1
  58.6 0.0 copy-done.2
  58.6 1.4 fusion.55
  60.0 0.0 copy-start
  60.0 3.4 %collective-permute-start.1 = (bf16[1,2048,512]{2,1,0:T(8,128)(2,1)S(1)}, bf16[1,2048,512]{2,1,0:T(8,128)(2,1)S(1)}, u32[]{:S(2)}, u32[]{:S(2)}) collective-permute-start(bf16[1,2048,512]{2,1,0:T(8,128)(2,1)S(1)} %get-tuple-element.6), channel_id=1, source_target_pairs={{0,32},{32,0},{16,48},{48,16},{64,96},{96,64},{80,112},{112,80},{1... | collective-permute-start | bytes 6291464 | tf_op jit(solution)/shard_map/ppermute | solution.py:31
  63.4 89.9 %collective-permute-done.1 = bf16[1,2048,512]{2,1,0:T(8,128)(2,1)S(1)} collective-permute-done((bf16[1,2048,512]{2,1,0:T(8,128)(2,1)S(1)}, bf16[1,2048,512]{2,1,0:T(8,128)(2,1)S(1)}, u32[]{:S(2)}, u32[]{:S(2)}) %collective-permute-start.1) | collective-permute-done | bytes 2097184 | tf_op jit(solution)/shard_map/ppermute | solution.py:31
  153.3 2.4 multiply_reduce_fusion.1
  155.6 0.0 copy-done
  157.0 4.5 %divide_convert_fusion.1 = (bf16[1,2048,512]{2,1,0:T(8,128)(2,1)}, bf16[1,2048,512]{2,1,0:T(8,128)(2,1)S(1)}) fusion(f32[1,2048,512]{2,1,0:T(8,128)} %copy-done, f32[]{:T(128)S(6)} %add.91, f32[]{:T(128)S(6)} %add.100, bf16[1,2048,512]{2,1,0:T(8,128)(2,1)S(1)} %collective-permute-done.1, bf16[2,1,1,2048,512]{4,3,2,1,0:T(8,128)(2,1)} %param.6), kind=kLoop, calls=%fused_computation.22 | loop fusion | flops 11534336 | bytes 12582920 | tf_op jit(solution)/shard_map/convert_element_type | solution.py:71
  161.5 0.0 copy-start.4
  161.5 1.3 copy-done.4
  162.8 1.3 fusion.46
  164.1 3.8 %fusion.4 = bf16[1,2048,512]{2,1,0:T(8,128)(2,1)S(1)} fusion(bf16[1,2048,512]{2,1,0:T(8,128)(2,1)} %copy-done.4, bf16[512,512]{1,0:T(8,128)(2,1)S(1)} %fusion.46), kind=kOutput, calls=%fused_computation.11 | convolution fusion | flops 1347682304 | bytes 4718592 | tf_op jit(solution)/shard_map/erc,ecd->erd/dot_general | solution.py:78
  168.0 1.3 fusion.49
  169.3 3.0 fusion.3
  172.2 3.5 %fusion.52 = bf16[512,512]{1,0:T(8,128)(2,1)S(1)} fusion(bf16[1,2048,512]{2,1,0:T(8,128)(2,1)} %fusion.3), kind=kOutput, calls=%fused_computation.65 | convolution fusion | flops 1074003968 | bytes 2621440 | tf_op jit(solution)/shard_map/erc,erd->ecd/dot_general | solution.py:73
  175.7 0.0 copy-start.3
  175.8 5.3 %fusion.2 = bf16[1,2048,512]{2,1,0:T(8,128)(2,1)} fusion(bf16[1,2048,512]{2,1,0:T(8,128)(2,1)} %fusion.3, bf16[512,512]{1,0:T(8,128)(2,1)S(1)} %fusion.52), kind=kOutput, calls=%fused_computation.7 | convolution fusion | flops 1347682304 | bytes 4718592 | tf_op jit(solution)/shard_map/erc,ecd->erd/dot_general | solution.py:78
  181.1 0.0 copy-done.3
  181.1 1.3 fusion.37
  182.3 2.9 fusion.7
  185.3 3.5 %fusion.40 = bf16[512,512]{1,0:T(8,128)(2,1)S(1)} fusion(bf16[1,2048,512]{2,1,0:T(8,128)(2,1)} %fusion.7), kind=kOutput, calls=%fused_computation.61 | convolution fusion | flops 1074003968 | bytes 2621440 | tf_op jit(solution)/shard_map/erc,erd->ecd/dot_general | solution.py:73
  188.8 3.8 %fusion.6 = bf16[1,2048,512]{2,1,0:T(8,128)(2,1)S(1)} fusion(bf16[1,2048,512]{2,1,0:T(8,128)(2,1)} %fusion.7, bf16[512,512]{1,0:T(8,128)(2,1)S(1)} %fusion.40), kind=kOutput, calls=%fused_computation.15 | convolution fusion | flops 1347682304 | bytes 4718592 | tf_op jit(solution)/shard_map/erc,ecd->erd/dot_general | solution.py:78
  192.6 0.0 copy-start.6
  192.6 1.3 copy-done.6
  193.9 1.3 fusion.43
  195.2 6.0 %fusion.1 = bf16[1,2048,512]{2,1,0:T(8,128)(2,1)S(1)} fusion(bf16[1,2048,512]{2,1,0:T(8,128)(2,1)} %param.4, bf16[1,2048,512]{2,1,0:T(8,128)(2,1)} %fusion.2, bf16[1,2048,512]{2,1,0:T(8,128)(2,1)} %copy-done.6, bf16[512,512]{1,0:T(8,128)(2,1)S(1)} %fusion.43), kind=kOutput, calls=%fused_computation.3 | convolution fusion | flops 1361313792 | bytes 8912896 | tf_op jit(solution)/shard_map/erc,ecd->erd/dot_general | solution.py:78
  201.2 0.0 copy-start.5
  201.2 1.5 copy.7
  202.8 0.0 reduce-scatter.3.cloned.1.call-update
  202.8 0.0 reduce-scatter.5.cloned.1.call-start
  202.8 44.4 %reduce-scatter.3.cloned.1.call-done = bf16[2,1,128,512]{3,2,1,0:T(8,128)(2,1)} async-done(((bf16[16,1,128,512]{3,2,1,0:T(8,128)(2,1)}), bf16[2,1,128,512]{3,2,1,0:T(8,128)(2,1)}) %reduce-scatter.3.cloned.1.call-update) | async-done | bytes 262160 | tf_op jit(solution)/shard_map/reduce_scatter | solution.py:40
  247.3 0.0 reduce-scatter.5.cloned.1.call-update
  247.3 17.4 %reduce-scatter.5.cloned.1.call-done = bf16[1,1,128,512]{3,2,1,0:T(8,128)(2,1)} async-done(((bf16[2,1,128,512]{3,2,1,0:T(8,128)(2,1)}), bf16[1,1,128,512]{3,2,1,0:T(8,128)(2,1)}) %reduce-scatter.5.cloned.1.call-update) | async-done | bytes 131088 | tf_op jit(solution)/shard_map/reduce_scatter | solution.py:40
  264.6 0.0 copy-done.5
  264.6 1.7 fusion.68
  266.4 0.2 broadcast_in_dim.5
  266.6 56.3 %all_to_all.5 = bf16[16,1,128,512]{3,2,1,0:T(8,128)(2,1)S(1)} all-to-all(bf16[16,1,128,512]{3,2,1,0:T(8,128)(2,1)S(1)} %broadcast_in_dim.5), channel_id=1, replica_groups=mesh['replica_0'=2,'replica_1'=8,'expert'=16] {'replica_0','replica_1'}, dimensions={0} | all-to-all | bytes 4194304 | tf_op jit(solution)/shard_map/all_to_all | solution.py:62
  322.9 1.3 copy.9
Async XLA Ops:
  7.2 240.1 %reduce-scatter.3.cloned.1.call-start = ((), (), s32[]{:S(2)}) async-start(), calls=%async_computation.3 | async-start | bytes 2359296 | tf_op jit(solution)/shard_map/reduce_scatter | solution.py:40
  7.2 51.4 %copy-start.1 = (bf16[2,1,1,2048,512]{4,3,2,1,0:T(8,128)(2,1)S(1)}, bf16[2,1,1,2048,512]{4,3,2,1,0:T(8,128)(2,1)}, u32[]{:S(2)}) copy-start(bf16[2,1,1,2048,512]{4,3,2,1,0:T(8,128)(2,1)} %param.6) | copy-start | bytes 12582916
  7.2 51.4 %copy-start.2 = (f32[1,1,2048,512]{3,2,1,0:T(8,128)S(1)}, f32[1,1,2048,512]{3,2,1,0:T(8,128)}, u32[]{:S(2)}) copy-start(f32[1,1,2048,512]{3,2,1,0:T(8,128)} %param.5) | copy-start | bytes 12582916
  11.0 47.6 %collective-permute-start = (bf16[1,2048,512]{2,1,0:T(8,128)(2,1)S(1)}, bf16[1,2048,512]{2,1,0:T(8,128)(2,1)S(1)}, u32[]{:S(2)}, u32[]{:S(2)}) collective-permute-start(bf16[1,2048,512]{2,1,0:T(8,128)(2,1)S(1)} %fusion.8), channel_id=1, source_target_pairs={{0,16},{16,0},{32,48},{48,32},{64,80},{80,64},{96,112},{112,96},{1... | collective-permute-start | bytes 6291464 | tf_op jit(solution)/shard_map/ppermute | solution.py:31
  60.0 95.6 %copy-start = (f32[1,2048,512]{2,1,0:T(8,128)}, f32[1,2048,512]{2,1,0:T(8,128)S(1)}, u32[]{:S(2)}) copy-start(f32[1,2048,512]{2,1,0:T(8,128)S(1)} %get-tuple-element.7) | copy-start | bytes 12582916
  60.0 93.2 %collective-permute-start.1 = (bf16[1,2048,512]{2,1,0:T(8,128)(2,1)S(1)}, bf16[1,2048,512]{2,1,0:T(8,128)(2,1)S(1)}, u32[]{:S(2)}, u32[]{:S(2)}) collective-permute-start(bf16[1,2048,512]{2,1,0:T(8,128)(2,1)S(1)} %get-tuple-element.6), channel_id=1, source_target_pairs={{0,32},{32,0},{16,48},{48,16},{64,96},{96,64},{80,112},{112,80},{1... | collective-permute-start | bytes 6291464 | tf_op jit(solution)/shard_map/ppermute | solution.py:31
  161.5 1.3 copy-start.4
  175.7 5.3 %copy-start.3 = (bf16[1,2048,512]{2,1,0:T(8,128)(2,1)S(1)}, bf16[1,2048,512]{2,1,0:T(8,128)(2,1)}, u32[]{:S(2)}) copy-start(bf16[1,2048,512]{2,1,0:T(8,128)(2,1)} %get-tuple-element.8) | copy-start | bytes 6291460
  192.6 1.3 copy-start.6
  201.2 63.4 %copy-start.5 = (f32[1,128,512]{2,1,0:T(8,128)S(1)}, f32[1,128,512]{2,1,0:T(8,128)}, u32[]{:S(2)}) copy-start(f32[1,128,512]{2,1,0:T(8,128)} %param.7) | copy-start | bytes 786436
  202.8 61.9 %reduce-scatter.5.cloned.1.call-start = ((), (), s32[]{:S(2)}) async-start(), calls=%async_computation.4 | async-start | bytes 393216 | tf_op jit(solution)/shard_map/reduce_scatter | solution.py:40
Sparse Core Ops, SparseCore 0:
  202.9 44.3 reduce-scatter.2
  249.7 14.8 reduce-scatter.4
where the time goes:
time: 332 us; the launch traced here: 331 us
  waiting for transfers between devices  197 us (59%)
  blocking collectives  56.3 us (17%)
  matrix products  37 us (11%)
  between operations  15.6 us (5%)
  other arithmetic  13.7 us (4%)
  local copies, waits for them, and re-layouts  5.73 us (2%)
  starting transfers between devices  5.44 us (2%)
    ppermute x2, waiting for transfers between devices, partner_2(): return lax.ppermute(block, axis, route)  136 us
    reduce_scatter x2, waiting for transfers between devices, reduced_to_own(): pieces = lax.psum_scatter(pieces, axes[k], scatter_dimension=0, tiled=True)  61.8 us
    all_to_all x1, blocking collectives, copy_for_each(): lax.all_to_all(jnp.broadcast_to(x[None], (devices, *x.shape)), axis, 0, 0...  56.3 us
    dot_general x6, matrix products, orthogonal(): jnp.einsum('erc,ecd->erd', current, poly, preferred_element_type=jnp.floa...  24.9 us
    dot_general x6, matrix products, orthogonal(): jnp.einsum('erc,erd->ecd', current, current, preferred_element_type=jnp.f...  12.1 us
  transfers between devices with their start and end apart: 4, of which 4 were waited for; matrix products, arithmetic and copies ran while one was open for 0% of the time, Pallas kernels for 0%

commit v1 on v0

v1 whole, which is shorter than its diff:
```python
import functools
import math

import jax
import jax.numpy as jnp
from jax import lax
from jax.experimental import pallas as pl
from jax.experimental.pallas import tpu as pltpu
from jax.sharding import PartitionSpec as P

A, B, C = 3.4445, -4.775, 2.0315
NZ = 8
MESH = pl.DeviceIdType.MESH
F32, BF16 = jnp.float32, jnp.bfloat16

CHUNK = 64
GROUP = 256
LAG = 3

STEPS_0 = (4, 3)
STEPS_1 = (3, 4)
X_ORDER = (4, 5, 3, 6, 2, 7, 1, 0)


def dot(a, b):
    return jnp.dot(a, b, preferred_element_type=F32)


def dot_t(a, b):
    return lax.dot_general(a, b, (((0,), (0,)), ((), ())), preferred_element_type=F32)


def split(a):
    high = a.astype(BF16)
    return high, (a - high.astype(F32)).astype(BF16)


def dot_3(a, b):
    return dot(a[0], b[0]) + dot(a[0], b[1]) + dot(a[1], b[0])


def kernel(
    scale, m_hbm, g_hbm, w_hbm, o_hbm, nw_hbm, no_hbm,
    m_v, g_v, w_v, o_v, no_v, out_v,
    a_in, b_in, a_out, b_out, x0, gram, d0, f_v, norm, e_v, xs, xr, r0, r1, rx,
    load_sem, small_sem, store_sem,
    a_recv, b_recv, ab_send,
    xr_recv, xr_send, r0_recv, r0_send, r1_recv, r1_send, rx_recv, rx_send,
    g0_recv, g0_send, g1_recv, g1_send, gx_recv, gx_send,
):
    rows, cols = m_v.shape
    half = cols // 2
    block = rows // (2 * NZ)
    chunks, groups, per = rows // CHUNK, rows // GROUP, GROUP // CHUNK
    me = lax.axis_index("replica")
    xl, z = me // NZ, lax.rem(me, NZ)
    over = (1 - xl) * NZ + z
    side = xl * NZ

    def at_z(offset):
        return lax.rem(z + offset + NZ, NZ)

    up, down = side + at_z(1), side + at_z(-1)
    q = lax.rem(z, 4)
    edge = jnp.logical_or(q == 0, q == 3)
    pair = side + z + 1 - 2 * lax.rem(z, 2)
    middle = side + lax.rem(jnp.where(q == 1, z + 1, z + NZ - 1), NZ)

    def send(src, dst, send_sem, recv_sem, to):
        return pltpu.make_async_remote_copy(
            src_ref=src, dst_ref=dst, send_sem=send_sem, recv_sem=recv_sem,
            device_id={"replica": to}, device_id_type=MESH,
        )

    def span(i, n):
        return pl.ds(pl.multiple_of(i * n, n), n)

    def load(i):
        s = span(i, GROUP)
        return (
            pltpu.make_async_copy(m_hbm.at[s], m_v.at[s], load_sem.at[0, i]),
            pltpu.make_async_copy(g_hbm.at[0, s], g_v.at[0, s], load_sem.at[1, i]),
            pltpu.make_async_copy(g_hbm.at[1, s], g_v.at[1, s], load_sem.at[2, i]),
        )

    for i in range(groups):
        for c in load(i):
            c.start()
    own_rows = span(me, block)
    small = (
        pltpu.make_async_copy(w_hbm.at[own_rows], w_v, small_sem.at[0]),
        pltpu.make_async_copy(o_hbm, o_v, small_sem.at[1]),
    )
    for c in small:
        c.start()

    barrier = pltpu.get_barrier_semaphore()
    for other in (up, down, over):
        pl.semaphore_signal(barrier, inc=1, device_id={"replica": other}, device_id_type=MESH)
    pl.semaphore_wait(barrier, 3)

    gram[...] = jnp.zeros_like(gram)
    norm[...] = jnp.zeros_like(norm)

    def moment(s):
        return 0.9 * m_v[s, :] + g_v[0, s, :].astype(F32)

    def send_a(i):
        s = span(i, CHUNK)
        return send(a_out.at[s], a_in.at[s], ab_send.at[0], a_recv.at[i], pair)

    def send_b(i):
        s = span(i, CHUNK)
        return send(b_out.at[s], b_in.at[s], ab_send.at[1], b_recv.at[i], middle)

    def keep(s, value):
        x0[s, :] = value.astype(BF16)
        squares = (value * value).reshape(CHUNK // 8, 8, cols)
        norm[...] += jnp.sum(squares, axis=0)

    def add_gram(j):
        x = x0[span(j, GROUP), :]
        gram[...] += dot_t(x, x)

    @pl.when(edge)
    def _():
        @pl.loop(0, groups)
        def _(j):
            for c in load(j):
                c.wait()
            for k in range(per):
                i = j * per + k
                s = span(i, CHUNK)
                a_out[s, :] = moment(s).astype(BF16)
                send_a(i).start()

        @pl.loop(0, groups)
        def _(j):
            for k in range(per):
                i = j * per + k
                s = span(i, CHUNK)
                send_a(i).wait_recv()
                keep(s, a_in[s, :].astype(F32) + 0.225 * moment(s) + 0.5 * g_v[1, s, :].astype(F32))
            add_gram(j)

        send(a_out, a_in, ab_send.at[0], a_recv.at[0], pair).wait_send()

    @pl.when(jnp.logical_not(edge))
    def _():
        def second(i):
            s = span(i, CHUNK)
            send_b(i).wait_recv()
            a_out[s, :] = (b_in[s, :].astype(F32) + 0.225 * moment(s)).astype(BF16)
            send_a(i).start()

        @pl.loop(0, groups)
        def _(j):
            for c in load(j):
                c.wait()
            for k in range(per):
                i = j * per + k
                s = span(i, CHUNK)
                send_a(i).wait_recv()
                mean = 0.5 * (a_in[s, :].astype(F32) + moment(s))
                b_out[s, :] = (0.45 * mean + 0.5 * g_v[1, s, :].astype(F32)).astype(BF16)
                send_b(i).start()
                keep(s, mean)
                if k >= LAG:
                    second(i - LAG)
                else:
                    pl.when(j > 0)(functools.partial(second, i - LAG))
            add_gram(j)

        for i in range(chunks - LAG, chunks):
            second(i)
        send(a_out, a_in, ab_send.at[0], a_recv.at[0], pair).wait_send()
        send(b_out, b_in, ab_send.at[1], b_recv.at[0], middle).wait_send()

    total = jnp.sum(jnp.sum(norm[...], axis=0, keepdims=True), axis=1, keepdims=True)
    unit = 1.0 / (jnp.sqrt(total) + 1e-7)

    g = gram[...] * (unit * unit)
    gs = split(g)
    d = B * g + C * dot(gs[0], gs[0])
    d0[...] = d
    ds = split(d)
    t = dot_3(gs, ds)
    gram[...] = (A * A) * g + (2 * A) * t + dot_3(split(t), ds)

    g = gram[...]
    gh = g.astype(BF16)
    d = B * g + C * dot(gh, gh)
    dh = d.astype(BF16)
    first = d0[...]
    f_v[...] = A * (first + d) + dot(first.astype(BF16), dh)
    t = dot(gh, dh)
    gram[...] = (A * A) * g + (2 * A) * t + dot(t.astype(BF16), dh)

    g = gram[...]
    gh = g.astype(BF16)
    d = B * g + C * dot(gh, gh)
    f = f_v[...]
    e = (A * A) * d + A * f + dot(f.astype(BF16), d.astype(BF16))
    factor = unit * scale
    e_v[...] = (e * factor).astype(BF16)
    lead = factor * (A * A * A)

    def row_block(k):
        return xl * NZ + at_z(k)

    def send_xr(k):
        zz = at_z(k)
        return send(xs.at[0, (1 - xl) * NZ + zz], xr.at[zz], xr_send.at[k], xr_recv.at[k], over)

    def slot(steps, way, t):
        return (0 if way > 0 else steps[0]) + t - 1

    def steps_of(steps, way):
        return steps[0] if way > 0 else steps[1]

    def towards(way):
        return up if way > 0 else down

    def x_of(jj):
        return 1 - xl if jj == 0 else xl

    def send_r0(way, t, src):
        i = slot(STEPS_0, way, t)
        return send(src, r0.at[i], r0_send.at[i], r0_recv.at[i], towards(way))

    def send_r1(jj, way, t, src):
        i = slot(STEPS_1, way, t)
        return send(src, r1.at[jj, i], r1_send.at[jj, i], r1_recv.at[jj, i], towards(way))

    def offset(way, n, t):
        return way * (n + 1 - t)

    sent = []
    e = e_v[...]
    for k in X_ORDER:
        zz = at_z(k)
        x = jnp.concatenate([x0[span(zz, block), :], x0[span(NZ + zz, block), :]], axis=0)
        y = (lead * x.astype(F32) + dot(x, e)).astype(BF16)
        for h in range(2):
            xs[h, zz] = y[:block, h * half : (h + 1) * half]
            xs[h, NZ + zz] = y[block:, h * half : (h + 1) * half]
        sent.append(send_xr(k))
        sent[-1].start()
        for way in (1, -1):
            n = steps_of(STEPS_1, way)
            if (way * n) % NZ == k:
                for jj in range(2):
                    sent.append(send_r1(jj, way, 1, xs.at[1, x_of(jj) * NZ + zz]))
                    sent[-1].start()

    def own_0(k):
        send_xr(k % NZ).wait_recv()
        zz = at_z(k)
        return zz, xs[0, side + zz].astype(F32) + xr[zz].astype(F32)

    def forward_0(way, t):
        n = steps_of(STEPS_0, way)
        i = slot(STEPS_0, way, t)
        send_r0(way, t, r0.at[i]).wait_recv()
        _, own = own_0(offset(way, n, t + 1))
        r0[i] = (r0[i].astype(F32) + own).astype(BF16)
        sent.append(send_r0(way, t + 1, r0.at[i]))
        sent[-1].start()

    def forward_1(jj, way, t):
        n = steps_of(STEPS_1, way)
        i = slot(STEPS_1, way, t)
        send_r1(jj, way, t, r1.at[jj, i]).wait_recv()
        own = xs[1, x_of(jj) * NZ + at_z(offset(way, n, t + 1))]
        r1[jj, i] = (r1[jj, i].astype(F32) + own.astype(F32)).astype(BF16)
        sent.append(send_r1(jj, way, t + 1, r1.at[jj, i]))
        sent[-1].start()

    for way in (1, -1):
        zz, own = own_0(offset(way, steps_of(STEPS_0, way), 1))
        xr[zz] = own.astype(BF16)
        sent.append(send_r0(way, 1, xr.at[zz]))
        sent[-1].start()
    for t in range(1, 4):
        for jj in range(2):
            for way in (1, -1):
                if t < steps_of(STEPS_1, way):
                    forward_1(jj, way, t)
        for way in (1, -1):
            if t < steps_of(STEPS_0, way):
                forward_0(way, t)

    def last_1(jj):
        out = xs[1, x_of(jj) * NZ + z].astype(F32)
        for way in (1, -1):
            i = slot(STEPS_1, way, steps_of(STEPS_1, way))
            send_r1(jj, way, steps_of(STEPS_1, way), r1.at[jj, i]).wait_recv()
            out += r1[jj, i].astype(F32)
        return out

    xs[1, (1 - xl) * NZ + z] = last_1(0).astype(BF16)
    cross = send(xs.at[1, (1 - xl) * NZ + z], rx, rx_send, rx_recv, over)
    cross.start()

    _, sum_0 = own_0(0)
    for way in (1, -1):
        n = steps_of(STEPS_0, way)
        i = slot(STEPS_0, way, n)
        send_r0(way, n, r0.at[i]).wait_recv()
        sum_0 += r0[i].astype(F32)

    for c in small:
        c.wait()

    def piece(b, h):
        return out_v.at[span(b, block), pl.ds(h * half, half)]

    def outer(h, delta):
        c = pl.ds(h * half, half)
        fresh = 0.9 * o_v[:, c] + delta
        no_v[:, c] = fresh
        out_v[own_rows, c] = (w_v[:, c].astype(F32) - fresh).astype(BF16)

    def send_g0(way, t):
        i = slot(STEPS_0, way, t)
        p = piece(side + at_z(-way * (t - 1)), 0)
        return send(p, p, g0_send.at[i], g0_recv.at[i], towards(way))

    def got_g0(way, t):
        i = slot(STEPS_0, way, t)
        p = piece(side + at_z(-way * t), 0)
        send(p, p, g0_send.at[i], g0_recv.at[i], towards(way)).wait_recv()

    def send_gx(k):
        p = piece(row_block(k), 0)
        return send(p, p, gx_send.at[k], gx_recv.at[k], over)

    def got_gx(k):
        p = piece((1 - xl) * NZ + at_z(k), 0)
        send(p, p, gx_send.at[k], gx_recv.at[k], over).wait_recv()

    def send_g1(jj, way, t):
        i = slot(STEPS_1, way, t)
        p = piece(x_of(jj) * NZ + at_z(-way * (t - 1)), 1)
        return send(p, p, g1_send.at[jj, i], g1_recv.at[jj, i], towards(way))

    def got_g1(jj, way, t):
        i = slot(STEPS_1, way, t)
        p = piece(x_of(jj) * NZ + at_z(-way * t), 1)
        send(p, p, g1_send.at[jj, i], g1_recv.at[jj, i], towards(way)).wait_recv()

    def go(c):
        sent.append(c)
        c.start()

    outer(0, sum_0)
    for way in (1, -1):
        go(send_g0(way, 1))
    go(send_gx(0))

    sum_1 = last_1(1)
    cross.wait_recv()
    outer(1, sum_1 + rx[...].astype(F32))
    p = piece(me, 1)
    go(send(p, p, gx_send.at[NZ], gx_recv.at[NZ], over))
    for way in (1, -1):
        go(send_g1(1, way, 1))
    store_outer = pltpu.make_async_copy(no_v, no_hbm, small_sem.at[2])
    store_outer.start()
    p = piece(over, 1)
    send(p, p, gx_send.at[NZ], gx_recv.at[NZ], over).wait_recv()
    for way in (1, -1):
        go(send_g1(0, way, 1))

    for t in range(1, 5):
        for way in (1, -1):
            n = steps_of(STEPS_0, way)
            if t <= n:
                got_g0(way, t)
                if t < n:
                    go(send_g0(way, t + 1))
                go(send_gx((-way * t) % NZ))
        for jj in (1, 0):
            for way in (1, -1):
                n = steps_of(STEPS_1, way)
                if t <= n:
                    got_g1(jj, way, t)
                    if t < n:
                        go(send_g1(jj, way, t + 1))
    for k in range(NZ):
        got_gx(k)

    store = pltpu.make_async_copy(out_v, nw_hbm, store_sem)
    store.start()
    for c in sent:
        c.wait_send()
    cross.wait_send()
    store_outer.wait()
    store.wait()


def per_device(weights, momentum, gradients, outer_momentum):
    rows, cols = weights.shape[1:]
    half, block = cols // 2, rows // (2 * NZ)
    chunks, groups = rows // CHUNK, rows // GROUP
    scale = 2 * 0.5 * 0.2 * math.sqrt(rows) / (2 * NZ)
    any_spec = pl.BlockSpec(memory_space=pl.ANY)
    dma = pltpu.SemaphoreType.DMA
    new_weights, new_outer = pl.pallas_call(
        functools.partial(kernel, scale),
        out_shape=(
            jax.ShapeDtypeStruct((rows, cols), BF16),
            jax.ShapeDtypeStruct((block, cols), F32),
        ),
        in_specs=[any_spec] * 4,
        out_specs=(any_spec, any_spec),
        scratch_shapes=[
            pltpu.VMEM((rows, cols), F32),
            pltpu.VMEM((2, rows, cols), BF16),
            pltpu.VMEM((block, cols), BF16),
            pltpu.VMEM((block, cols), F32),
            pltpu.VMEM((block, cols), F32),
            pltpu.VMEM((rows, cols), BF16),
            pltpu.VMEM((rows, cols), BF16),
            pltpu.VMEM((rows, cols), BF16),
            pltpu.VMEM((rows, cols), BF16),
            pltpu.VMEM((rows, cols), BF16),
            pltpu.VMEM((rows, cols), BF16),
            pltpu.VMEM((cols, cols), F32),
            pltpu.VMEM((cols, cols), F32),
            pltpu.VMEM((cols, cols), F32),
            pltpu.VMEM((8, cols), F32),
            pltpu.VMEM((cols, cols), BF16),
            pltpu.VMEM((2, 2 * NZ, block, half), BF16),
            pltpu.VMEM((NZ, block, half), BF16),
            pltpu.VMEM((NZ - 1, block, half), BF16),
            pltpu.VMEM((2, NZ - 1, block, half), BF16),
            pltpu.VMEM((block, half), BF16),
            dma((3, groups)),
            dma((3,)),
            dma,
            dma((chunks,)), dma((chunks,)), dma((2,)),
            dma((NZ,)), dma((NZ,)),
            dma((NZ - 1,)), dma((NZ - 1,)),
            dma((2, NZ - 1)), dma((2, NZ - 1)),
            dma, dma,
            dma((NZ - 1,)), dma((NZ - 1,)),
            dma((2, NZ - 1)), dma((2, NZ - 1)),
            dma((NZ + 1,)), dma((NZ + 1,)),
        ],
        compiler_params=pltpu.CompilerParams(
            collective_id=0, has_side_effects=True, vmem_limit_bytes=56 * 1024 * 1024
        ),
        name="gossip_muon",
    )(momentum[0, 0], gradients[:, 0, 0], weights[0], outer_momentum[0])
    return new_weights[None], new_outer[None]


def solution(mesh):
    return jax.shard_map(
        per_device,
        mesh=mesh,
        in_specs=(
            P("expert", None, None),
            P("replica", "expert", None, None),
            P(None, "replica", "expert", None, None),
            P("expert", "replica", None),
        ),
        out_specs=(P("expert", None, None), P("expert", "replica", None)),
        check_vma=False,
    )
```

time: 332 us -> 114 us (0.34)
  waiting for transfers between devices: 197 us -> 0 us
  Pallas kernels: 0 us -> 110 us
  blocking collectives: 56.3 us -> 0 us
  matrix products: 37 us -> 0 us
  between operations: 15.6 us -> 0.65 us
  other arithmetic: 13.7 us -> 0 us
  starting transfers between devices: 5.44 us -> 0 us
    ppermute x2 -> x0, waiting for transfers between devices: 136 us -> none  [partner_2(): return lax.ppermute(block, axis, route)]
    pallas_call x0 -> x1, Pallas kernels: none -> 110 us  [per_device(): pl.pallas_call(functools.partial(kernel, scale), out_shape=(jax.ShapeDtyp...]
    reduce_scatter x2 -> x0, waiting for transfers between devices: 61.8 us -> none  [reduced_to_own(): pieces = lax.psum_scatter(pieces, axes[k], scatter_dimension=0, tiled=True)]
    all_to_all x1 -> x0, blocking collectives: 56.3 us -> none  [copy_for_each(): lax.all_to_all(jnp.broadcast_to(x[None], (devices, *x.shape)), axis, 0, 0...]
    dot_general x12 -> x0, matrix products: 37 us -> none  [the longest x6 24.9 us: orthogonal(): jnp.einsum('erc,ecd->erd', current, poly, preferred_element_type=jnp.floa...]
    convert_element_type x3 -> x0, other arithmetic: 9.62 us -> none  [the longest x2 5.12 us: per_device(): moment.astype(jnp.bfloat16)]
    ppermute x2 -> x0, starting transfers between devices: 5.36 us -> none  [partner_2(): return lax.ppermute(block, axis, route)]
  transfers between devices with their start and end apart: 4 -> 0, of which waited for: 4 -> 0; matrix products, arithmetic and copies ran while one was open for 0% -> 0% of each run, Pallas kernels for 0% -> 0%
where the time goes in v1:
time: 114 us
  Pallas kernels  110 us (96%)
  local copies, waits for them, and re-layouts  3.79 us (3%)
    pallas_call x1, Pallas kernels, per_device(): pl.pallas_call(functools.partial(kernel, scale), out_shape=(jax.ShapeDtyp...  110 us
    unnamed x4, local copies, waits for them, and re-layouts  3.79 us

profile of v1, /device:TPU:10, one launch (start us, length us, event | category | flops | bytes accessed | tf_op | source)
XLA Modules:
  0.0 114.2 jit_solution(4833767885667304212)
XLA Ops:
  0.6 109.8 %gossip_muon.1 = (bf16[2048,512]{1,0:T(8,128)(2,1)}, f32[128,512]{1,0:T(8,128)}) custom-call(f32[2048,512]{1,0:T(8,128)} %bitcast.6, bf16[2,2048,512]{2,1,0:T(8,128)(2,1)} %bitcast.7, bf16[2048,512]{1,0:T(8,128)(2,1)} %bitcast.9, f32[128,512]{1,0:T(8,128)} %bitcast.11), custom_call_target="tpu_custom_call" | custom-call | tf_op jit(solution)/shard_map/gossip_muon/pallas_call | solution.py:409
  110.4 0.0 copy-start
  110.4 3.1 %copy.8 = bf16[1,2048,512]{2,1,0:T(8,128)(2,1)} copy(bf16[1,2048,512]{2,1,0:T(8,128)(2,1)} %bitcast.8) | data formatting | bytes 4194304
  113.5 0.0 copy-done
  113.5 0.7 copy.9
Async XLA Ops:
  110.4 3.1 %copy-start = (f32[128,512]{1,0:T(8,128)S(1)}, f32[128,512]{1,0:T(8,128)}, u32[]{:S(2)}) copy-start(f32[128,512]{1,0:T(8,128)} %get-tuple-element.5) | copy-start | bytes 786436

commit v2 on v1

--- a/solution.py
+++ b/solution.py
@@ -13,9 +13,9 @@
 MESH = pl.DeviceIdType.MESH
 F32, BF16 = jnp.float32, jnp.bfloat16
 
-CHUNK = 64
+CHUNK = 32
 GROUP = 256
-LAG = 3
+LAG = 4
 
 STEPS_0 = (4, 3)
 STEPS_1 = (3, 4)
@@ -30,20 +30,11 @@
     return lax.dot_general(a, b, (((0,), (0,)), ((), ())), preferred_element_type=F32)
 
 
-def split(a):
-    high = a.astype(BF16)
-    return high, (a - high.astype(F32)).astype(BF16)
-
-
-def dot_3(a, b):
-    return dot(a[0], b[0]) + dot(a[0], b[1]) + dot(a[1], b[0])
-
-
 def kernel(
-    scale, m_hbm, g_hbm, w_hbm, o_hbm, nw_hbm, no_hbm,
-    m_v, g_v, w_v, o_v, no_v, out_v,
+    scale, m_hbm, g_hbm, w_hbm, o_hbm, out_v, no_v,
+    m_v, g_v, w_v, o_v,
     a_in, b_in, a_out, b_out, x0, gram, d0, f_v, norm, e_v, xs, xr, r0, r1, rx,
-    load_sem, small_sem, store_sem,
+    load_sem, small_sem,
     a_recv, b_recv, ab_send,
     xr_recv, xr_send, r0_recv, r0_send, r1_recv, r1_send, rx_recv, rx_send,
     g0_recv, g0_send, g1_recv, g1_send, gx_recv, gx_send,
@@ -142,8 +133,6 @@
                 send_a(i).wait_recv()
                 keep(s, a_in[s, :].astype(F32) + 0.225 * moment(s) + 0.5 * g_v[1, s, :].astype(F32))
             add_gram(j)
-
-        send(a_out, a_in, ab_send.at[0], a_recv.at[0], pair).wait_send()
 
     @pl.when(jnp.logical_not(edge))
     def _():
@@ -173,19 +162,17 @@
 
         for i in range(chunks - LAG, chunks):
             second(i)
-        send(a_out, a_in, ab_send.at[0], a_recv.at[0], pair).wait_send()
-        send(b_out, b_in, ab_send.at[1], b_recv.at[0], middle).wait_send()
 
     total = jnp.sum(jnp.sum(norm[...], axis=0, keepdims=True), axis=1, keepdims=True)
     unit = 1.0 / (jnp.sqrt(total) + 1e-7)
 
     g = gram[...] * (unit * unit)
-    gs = split(g)
-    d = B * g + C * dot(gs[0], gs[0])
+    gh = g.astype(BF16)
+    d = B * g + C * dot(gh, gh)
     d0[...] = d
-    ds = split(d)
-    t = dot_3(gs, ds)
-    gram[...] = (A * A) * g + (2 * A) * t + dot_3(split(t), ds)
+    dh = d.astype(BF16)
+    t = dot(gh, dh)
+    gram[...] = (A * A) * g + (2 * A) * t + dot(t.astype(BF16), dh)
 
     g = gram[...]
     gh = g.astype(BF16)
@@ -365,8 +352,6 @@
     go(send(p, p, gx_send.at[NZ], gx_recv.at[NZ], over))
     for way in (1, -1):
         go(send_g1(1, way, 1))
-    store_outer = pltpu.make_async_copy(no_v, no_hbm, small_sem.at[2])
-    store_outer.start()
     p = piece(over, 1)
     send(p, p, gx_send.at[NZ], gx_recv.at[NZ], over).wait_recv()
     for way in (1, -1):
@@ -390,13 +375,25 @@
     for k in range(NZ):
         got_gx(k)
 
-    store = pltpu.make_async_copy(out_v, nw_hbm, store_sem)
-    store.start()
     for c in sent:
         c.wait_send()
     cross.wait_send()
-    store_outer.wait()
-    store.wait()
+    send(a_out, a_in, ab_send.at[0], a_recv.at[0], pair).wait_send()
+
+    @pl.when(jnp.logical_not(edge))
+    def _():
+        send(b_out, b_in, ab_send.at[1], b_recv.at[0], middle).wait_send()
+
+
+def write_out(w_v, o_v, w_hbm, o_hbm, sem):
+    copies = (
+        pltpu.make_async_copy(w_v, w_hbm, sem.at[0]),
+        pltpu.make_async_copy(o_v, o_hbm, sem.at[1]),
+    )
+    for c in copies:
+        c.start()
+    for c in copies:
+        c.wait()
 
 
 def per_device(weights, momentum, gradients, outer_momentum):
@@ -404,23 +401,20 @@
     half, block = cols // 2, rows // (2 * NZ)
     chunks, groups = rows // CHUNK, rows // GROUP
     scale = 2 * 0.5 * 0.2 * math.sqrt(rows) / (2 * NZ)
+    hbm_spec = pl.BlockSpec(memory_space=pltpu.HBM)
     any_spec = pl.BlockSpec(memory_space=pl.ANY)
+    vmem_spec = pl.BlockSpec(memory_space=pltpu.VMEM)
     dma = pltpu.SemaphoreType.DMA
     new_weights, new_outer = pl.pallas_call(
         functools.partial(kernel, scale),
-        out_shape=(
-            jax.ShapeDtypeStruct((rows, cols), BF16),
-            jax.ShapeDtypeStruct((block, cols), F32),
-        ),
-        in_specs=[any_spec] * 4,
-        out_specs=(any_spec, any_spec),
+        out_shape=(pltpu.VMEM((rows, cols), BF16), pltpu.VMEM((block, cols), F32)),
+        in_specs=[hbm_spec] * 4,
+        out_specs=(vmem_spec, vmem_spec),
         scratch_shapes=[
             pltpu.VMEM((rows, cols), F32),
             pltpu.VMEM((2, rows, cols), BF16),
             pltpu.VMEM((block, cols), BF16),
             pltpu.VMEM((block, cols), F32),
-            pltpu.VMEM((block, cols), F32),
-            pltpu.VMEM((rows, cols), BF16),
             pltpu.VMEM((rows, cols), BF16),
             pltpu.VMEM((rows, cols), BF16),
             pltpu.VMEM((rows, cols), BF16),
@@ -437,8 +431,7 @@
             pltpu.VMEM((2, NZ - 1, block, half), BF16),
             pltpu.VMEM((block, half), BF16),
             dma((3, groups)),
-            dma((3,)),
-            dma,
+            dma((2,)),
             dma((chunks,)), dma((chunks,)), dma((2,)),
             dma((NZ,)), dma((NZ,)),
             dma((NZ - 1,)), dma((NZ - 1,)),
@@ -449,10 +442,27 @@
             dma((NZ + 1,)), dma((NZ + 1,)),
         ],
         compiler_params=pltpu.CompilerParams(
-            collective_id=0, has_side_effects=True, vmem_limit_bytes=56 * 1024 * 1024
+            collective_id=0, has_side_effects=True, vmem_limit_bytes=48 * 1024 * 1024
         ),
         name="gossip_muon",
-    )(momentum[0, 0], gradients[:, 0, 0], weights[0], outer_momentum[0])
+    )(*(
+        pltpu.with_memory_space_constraint(a, pltpu.HBM)
+        for a in (momentum[0, 0], gradients[:, 0, 0], weights[0], outer_momentum[0])
+    ))
+    new_weights, new_outer = pl.pallas_call(
+        write_out,
+        out_shape=(
+            jax.ShapeDtypeStruct((rows, cols), BF16),
+            jax.ShapeDtypeStruct((block, cols), F32),
+        ),
+        in_specs=[vmem_spec] * 2,
+        out_specs=(any_spec, any_spec),
+        scratch_shapes=[dma((2,))],
+        name="write_out",
+    )(
+        pltpu.with_memory_space_constraint(new_weights, pltpu.VMEM),
+        pltpu.with_memory_space_constraint(new_outer, pltpu.VMEM),
+    )
     return new_weights[None], new_outer[None]
 
 

time: 114 us -> 109 us (0.956)
  local copies, waits for them, and re-layouts: 3.79 us -> 0 us
  Pallas kernels: 110 us -> 108 us
    unnamed x4 -> x0, local copies, waits for them, and re-layouts: 3.79 us -> none
    pallas_call x1 -> x2, Pallas kernels: 110 us -> 108 us  [the longest x1 106 us: per_device(): pl.pallas_call(functools.partial(kernel, scale), out_shape=(pltpu.VMEM((r...]
where the time goes in v2:
time: 109 us; the launch traced here: 108 us
  Pallas kernels  108 us (99%)
    pallas_call x1, Pallas kernels, per_device(): pl.pallas_call(functools.partial(kernel, scale), out_shape=(pltpu.VMEM((r...  106 us

profile of v2, /device:TPU:10, one launch (start us, length us, event | category | flops | bytes accessed | tf_op | source)
XLA Modules:
  0.0 108.3 jit_solution(39364298747919595)
XLA Ops:
  0.6 106.2 %gossip_muon.1 = (bf16[2048,512]{1,0:T(8,128)(2,1)S(1)}, f32[128,512]{1,0:T(8,128)S(1)}) custom-call(f32[2048,512]{1,0:T(8,128)} %bitcast.6, bf16[2,2048,512]{2,1,0:T(8,128)(2,1)} %bitcast.7, bf16[2048,512]{1,0:T(8,128)(2,1)} %bitcast.8, f32[128,512]{1,0:T(8,128)} %bitcast.9), custom_call_target="tpu_custom_call" | custom-call | tf_op jit(solution)/shard_map/gossip_muon/pallas_call | solution.py:408
  106.8 1.4 %write_out.1 = (bf16[2048,512]{1,0:T(8,128)(2,1)}, f32[128,512]{1,0:T(8,128)}) custom-call(bf16[2048,512]{1,0:T(8,128)(2,1)S(1)} %get-tuple-element.6.w_v, f32[128,512]{1,0:T(8,128)S(1)} %get-tuple-element.7.o_v), custom_call_target="tpu_custom_call" | custom-call | tf_op jit(solution)/shard_map/write_out/pallas_call | solution.py:452

commit v3 on v2

--- a/solution.py
+++ b/solution.py
@@ -19,6 +19,7 @@
 
 STEPS_0 = (4, 3)
 STEPS_1 = (3, 4)
+WAVES = 2
 X_ORDER = (4, 5, 3, 6, 2, 7, 1, 0)
 
 
@@ -42,6 +43,7 @@
     rows, cols = m_v.shape
     half = cols // 2
     block = rows // (2 * NZ)
+    part = block // WAVES
     chunks, groups, per = rows // CHUNK, rows // GROUP, GROUP // CHUNK
     me = lax.axis_index("replica")
     xl, z = me // NZ, lax.rem(me, NZ)
@@ -192,12 +194,10 @@
     e_v[...] = (e * factor).astype(BF16)
     lead = factor * (A * A * A)
 
-    def row_block(k):
-        return xl * NZ + at_z(k)
-
-    def send_xr(k):
+    def send_xr(v, k):
         zz = at_z(k)
-        return send(xs.at[0, (1 - xl) * NZ + zz], xr.at[zz], xr_send.at[k], xr_recv.at[k], over)
+        src = xs.at[0, v, (1 - xl) * NZ + zz]
+        return send(src, xr.at[v, zz], xr_send.at[v, k], xr_recv.at[v, k], over)
 
     def slot(steps, way, t):
         return (0 if way > 0 else steps[0]) + t - 1
@@ -211,173 +211,197 @@
     def x_of(jj):
         return 1 - xl if jj == 0 else xl
 
-    def send_r0(way, t, src):
+    def send_r0(v, way, t, src):
         i = slot(STEPS_0, way, t)
-        return send(src, r0.at[i], r0_send.at[i], r0_recv.at[i], towards(way))
-
-    def send_r1(jj, way, t, src):
+        return send(src, r0.at[v, i], r0_send.at[v, i], r0_recv.at[v, i], towards(way))
+
+    def send_r1(v, jj, way, t, src):
         i = slot(STEPS_1, way, t)
-        return send(src, r1.at[jj, i], r1_send.at[jj, i], r1_recv.at[jj, i], towards(way))
+        return send(src, r1.at[v, jj, i], r1_send.at[v, jj, i], r1_recv.at[v, jj, i], towards(way))
 
     def offset(way, n, t):
         return way * (n + 1 - t)
 
     sent = []
+
+    def go(c):
+        sent.append(c)
+        c.start()
+
     e = e_v[...]
     for k in X_ORDER:
         zz = at_z(k)
         x = jnp.concatenate([x0[span(zz, block), :], x0[span(NZ + zz, block), :]], axis=0)
         y = (lead * x.astype(F32) + dot(x, e)).astype(BF16)
-        for h in range(2):
-            xs[h, zz] = y[:block, h * half : (h + 1) * half]
-            xs[h, NZ + zz] = y[block:, h * half : (h + 1) * half]
-        sent.append(send_xr(k))
-        sent[-1].start()
-        for way in (1, -1):
-            n = steps_of(STEPS_1, way)
-            if (way * n) % NZ == k:
-                for jj in range(2):
-                    sent.append(send_r1(jj, way, 1, xs.at[1, x_of(jj) * NZ + zz]))
-                    sent[-1].start()
-
-    def own_0(k):
-        send_xr(k % NZ).wait_recv()
+        for v in range(WAVES):
+            for h in range(2):
+                c = slice(h * half, (h + 1) * half)
+                xs[h, v, zz] = y[v * part : (v + 1) * part, c]
+                xs[h, v, NZ + zz] = y[block + v * part : block + (v + 1) * part, c]
+        for v in range(WAVES):
+            go(send_xr(v, k))
+            for way in (1, -1):
+                n = steps_of(STEPS_1, way)
+                if (way * n) % NZ == k:
+                    for jj in range(2):
+                        go(send_r1(v, jj, way, 1, xs.at[1, v, x_of(jj) * NZ + zz]))
+
+    def own_0(v, k):
+        send_xr(v, k % NZ).wait_recv()
         zz = at_z(k)
-        return zz, xs[0, side + zz].astype(F32) + xr[zz].astype(F32)
-
-    def forward_0(way, t):
+        return zz, xs[0, v, side + zz].astype(F32) + xr[v, zz].astype(F32)
+
+    def first_0(v):
+        for way in (1, -1):
+            zz, own = own_0(v, offset(way, steps_of(STEPS_0, way), 1))
+            xr[v, zz] = own.astype(BF16)
+            go(send_r0(v, way, 1, xr.at[v, zz]))
+
+    def forward_0(v, way, t):
         n = steps_of(STEPS_0, way)
         i = slot(STEPS_0, way, t)
-        send_r0(way, t, r0.at[i]).wait_recv()
-        _, own = own_0(offset(way, n, t + 1))
-        r0[i] = (r0[i].astype(F32) + own).astype(BF16)
-        sent.append(send_r0(way, t + 1, r0.at[i]))
-        sent[-1].start()
-
-    def forward_1(jj, way, t):
+        send_r0(v, way, t, r0.at[v, i]).wait_recv()
+        _, own = own_0(v, offset(way, n, t + 1))
+        r0[v, i] = (r0[v, i].astype(F32) + own).astype(BF16)
+        go(send_r0(v, way, t + 1, r0.at[v, i]))
+
+    def forward_1(v, jj, way, t):
         n = steps_of(STEPS_1, way)
         i = slot(STEPS_1, way, t)
-        send_r1(jj, way, t, r1.at[jj, i]).wait_recv()
-        own = xs[1, x_of(jj) * NZ + at_z(offset(way, n, t + 1))]
-        r1[jj, i] = (r1[jj, i].astype(F32) + own.astype(F32)).astype(BF16)
-        sent.append(send_r1(jj, way, t + 1, r1.at[jj, i]))
-        sent[-1].start()
-
-    for way in (1, -1):
-        zz, own = own_0(offset(way, steps_of(STEPS_0, way), 1))
-        xr[zz] = own.astype(BF16)
-        sent.append(send_r0(way, 1, xr.at[zz]))
-        sent[-1].start()
-    for t in range(1, 4):
+        send_r1(v, jj, way, t, r1.at[v, jj, i]).wait_recv()
+        own = xs[1, v, x_of(jj) * NZ + at_z(offset(way, n, t + 1))]
+        r1[v, jj, i] = (r1[v, jj, i].astype(F32) + own.astype(F32)).astype(BF16)
+        go(send_r1(v, jj, way, t + 1, r1.at[v, jj, i]))
+
+    def reduce_step(v, t):
         for jj in range(2):
             for way in (1, -1):
                 if t < steps_of(STEPS_1, way):
-                    forward_1(jj, way, t)
+                    forward_1(v, jj, way, t)
         for way in (1, -1):
             if t < steps_of(STEPS_0, way):
-                forward_0(way, t)
-
-    def last_1(jj):
-        out = xs[1, x_of(jj) * NZ + z].astype(F32)
-        for way in (1, -1):
-            i = slot(STEPS_1, way, steps_of(STEPS_1, way))
-            send_r1(jj, way, steps_of(STEPS_1, way), r1.at[jj, i]).wait_recv()
-            out += r1[jj, i].astype(F32)
+                forward_0(v, way, t)
+
+    def last_1(v, jj):
+        out = xs[1, v, x_of(jj) * NZ + z].astype(F32)
+        for way in (1, -1):
+            n = steps_of(STEPS_1, way)
+            i = slot(STEPS_1, way, n)
+            send_r1(v, jj, way, n, r1.at[v, jj, i]).wait_recv()
+            out += r1[v, jj, i].astype(F32)
         return out
 
-    xs[1, (1 - xl) * NZ + z] = last_1(0).astype(BF16)
-    cross = send(xs.at[1, (1 - xl) * NZ + z], rx, rx_send, rx_recv, over)
-    cross.start()
-
-    _, sum_0 = own_0(0)
-    for way in (1, -1):
-        n = steps_of(STEPS_0, way)
-        i = slot(STEPS_0, way, n)
-        send_r0(way, n, r0.at[i]).wait_recv()
-        sum_0 += r0[i].astype(F32)
-
-    for c in small:
-        c.wait()
-
-    def piece(b, h):
-        return out_v.at[span(b, block), pl.ds(h * half, half)]
-
-    def outer(h, delta):
-        c = pl.ds(h * half, half)
-        fresh = 0.9 * o_v[:, c] + delta
-        no_v[:, c] = fresh
-        out_v[own_rows, c] = (w_v[:, c].astype(F32) - fresh).astype(BF16)
-
-    def send_g0(way, t):
+    def last_0(v):
+        _, out = own_0(v, 0)
+        for way in (1, -1):
+            n = steps_of(STEPS_0, way)
+            i = slot(STEPS_0, way, n)
+            send_r0(v, way, n, r0.at[v, i]).wait_recv()
+            out += r0[v, i].astype(F32)
+        return out
+
+    def cross(v):
+        src = xs.at[1, v, (1 - xl) * NZ + z]
+        return send(src, rx.at[v], rx_send.at[v], rx_recv.at[v], over)
+
+    def rows_of(v, b):
+        return pl.ds(pl.multiple_of(b * block + v * part, part), part)
+
+    def piece(v, b, h):
+        return out_v.at[rows_of(v, b), pl.ds(h * half, half)]
+
+    def outer(v, h, delta):
+        r, c = slice(v * part, (v + 1) * part), slice(h * half, (h + 1) * half)
+        fresh = 0.9 * o_v[r, c] + delta
+        no_v[r, c] = fresh
+        out_v[rows_of(v, me), c] = (w_v[r, c].astype(F32) - fresh).astype(BF16)
+
+    def send_g0(v, way, t, p):
         i = slot(STEPS_0, way, t)
-        p = piece(side + at_z(-way * (t - 1)), 0)
-        return send(p, p, g0_send.at[i], g0_recv.at[i], towards(way))
-
-    def got_g0(way, t):
-        i = slot(STEPS_0, way, t)
-        p = piece(side + at_z(-way * t), 0)
-        send(p, p, g0_send.at[i], g0_recv.at[i], towards(way)).wait_recv()
-
-    def send_gx(k):
-        p = piece(row_block(k), 0)
-        return send(p, p, gx_send.at[k], gx_recv.at[k], over)
-
-    def got_gx(k):
-        p = piece((1 - xl) * NZ + at_z(k), 0)
-        send(p, p, gx_send.at[k], gx_recv.at[k], over).wait_recv()
-
-    def send_g1(jj, way, t):
+        return send(p, p, g0_send.at[v, i], g0_recv.at[v, i], towards(way))
+
+    def send_g1(v, jj, way, t, p):
         i = slot(STEPS_1, way, t)
-        p = piece(x_of(jj) * NZ + at_z(-way * (t - 1)), 1)
-        return send(p, p, g1_send.at[jj, i], g1_recv.at[jj, i], towards(way))
-
-    def got_g1(jj, way, t):
-        i = slot(STEPS_1, way, t)
-        p = piece(x_of(jj) * NZ + at_z(-way * t), 1)
-        send(p, p, g1_send.at[jj, i], g1_recv.at[jj, i], towards(way)).wait_recv()
-
-    def go(c):
-        sent.append(c)
-        c.start()
-
-    outer(0, sum_0)
-    for way in (1, -1):
-        go(send_g0(way, 1))
-    go(send_gx(0))
-
-    sum_1 = last_1(1)
-    cross.wait_recv()
-    outer(1, sum_1 + rx[...].astype(F32))
-    p = piece(me, 1)
-    go(send(p, p, gx_send.at[NZ], gx_recv.at[NZ], over))
-    for way in (1, -1):
-        go(send_g1(1, way, 1))
-    p = piece(over, 1)
-    send(p, p, gx_send.at[NZ], gx_recv.at[NZ], over).wait_recv()
-    for way in (1, -1):
-        go(send_g1(0, way, 1))
-
-    for t in range(1, 5):
+        return send(p, p, g1_send.at[v, jj, i], g1_recv.at[v, jj, i], towards(way))
+
+    def send_gx(v, k, p):
+        return send(p, p, gx_send.at[v, k], gx_recv.at[v, k], over)
+
+    def gather_0(v, t):
         for way in (1, -1):
             n = steps_of(STEPS_0, way)
             if t <= n:
-                got_g0(way, t)
+                k = (-way * t) % NZ
+                p = piece(v, side + at_z(k), 0)
+                send_g0(v, way, t, p).wait_recv()
                 if t < n:
-                    go(send_g0(way, t + 1))
-                go(send_gx((-way * t) % NZ))
+                    go(send_g0(v, way, t + 1, p))
+                go(send_gx(v, k, p))
+
+    def gather_1(v, t):
         for jj in (1, 0):
             for way in (1, -1):
                 n = steps_of(STEPS_1, way)
                 if t <= n:
-                    got_g1(jj, way, t)
+                    p = piece(v, x_of(jj) * NZ + at_z(-way * t), 1)
+                    send_g1(v, jj, way, t, p).wait_recv()
                     if t < n:
-                        go(send_g1(jj, way, t + 1))
-    for k in range(NZ):
-        got_gx(k)
+                        go(send_g1(v, jj, way, t + 1, p))
+
+    def end_a(v):
+        xs[1, v, (1 - xl) * NZ + z] = last_1(v, 0).astype(BF16)
+        go(cross(v))
+        outer(v, 0, last_0(v))
+        p = piece(v, me, 0)
+        for way in (1, -1):
+            go(send_g0(v, way, 1, p))
+        go(send_gx(v, 0, p))
+
+    def end_b(v):
+        total_1 = last_1(v, 1)
+        cross(v).wait_recv()
+        outer(v, 1, total_1 + rx[v].astype(F32))
+        p = piece(v, me, 1)
+        go(send_gx(v, NZ, p))
+        for way in (1, -1):
+            go(send_g1(v, 1, way, 1, p))
+
+    def end_c(v):
+        p = piece(v, over, 1)
+        send_gx(v, NZ, p).wait_recv()
+        for way in (1, -1):
+            go(send_g1(v, 0, way, 1, p))
+
+    def both(step, *args):
+        for v in range(WAVES):
+            step(v, *args)
+
+    both(first_0)
+    for t in range(1, 4):
+        both(reduce_step, t)
+    for c in small:
+        c.wait()
+    both(end_a)
+    end_b(0)
+    both(gather_0, 1)
+    for v in range(1, WAVES):
+        end_b(v)
+    end_c(0)
+    both(gather_0, 2)
+    for v in range(1, WAVES):
+        end_c(v)
+    both(gather_1, 1)
+    both(gather_0, 3)
+    both(gather_1, 2)
+    both(gather_0, 4)
+    both(gather_1, 3)
+    both(gather_1, 4)
+    for v in range(WAVES):
+        for k in range(NZ):
+            send_gx(v, k, piece(v, (1 - xl) * NZ + at_z(k), 0)).wait_recv()
 
     for c in sent:
         c.wait_send()
-    cross.wait_send()
     send(a_out, a_in, ab_send.at[0], a_recv.at[0], pair).wait_send()
 
     @pl.when(jnp.logical_not(edge))
@@ -399,6 +423,7 @@
 def per_device(weights, momentum, gradients, outer_momentum):
     rows, cols = weights.shape[1:]
     half, block = cols // 2, rows // (2 * NZ)
+    part = block // WAVES
     chunks, groups = rows // CHUNK, rows // GROUP
     scale = 2 * 0.5 * 0.2 * math.sqrt(rows) / (2 * NZ)
     hbm_spec = pl.BlockSpec(memory_space=pltpu.HBM)
@@ -425,21 +450,21 @@
             pltpu.VMEM((cols, cols), F32),
             pltpu.VMEM((8, cols), F32),
             pltpu.VMEM((cols, cols), BF16),
-            pltpu.VMEM((2, 2 * NZ, block, half), BF16),
-            pltpu.VMEM((NZ, block, half), BF16),
-            pltpu.VMEM((NZ - 1, block, half), BF16),
-            pltpu.VMEM((2, NZ - 1, block, half), BF16),
-            pltpu.VMEM((block, half), BF16),
+            pltpu.VMEM((2, WAVES, 2 * NZ, part, half), BF16),
+            pltpu.VMEM((WAVES, NZ, part, half), BF16),
+            pltpu.VMEM((WAVES, NZ - 1, part, half), BF16),
+            pltpu.VMEM((WAVES, 2, NZ - 1, part, half), BF16),
+            pltpu.VMEM((WAVES, part, half), BF16),
             dma((3, groups)),
             dma((2,)),
             dma((chunks,)), dma((chunks,)), dma((2,)),
-            dma((NZ,)), dma((NZ,)),
-            dma((NZ - 1,)), dma((NZ - 1,)),
-            dma((2, NZ - 1)), dma((2, NZ - 1)),
-            dma, dma,
-            dma((NZ - 1,)), dma((NZ - 1,)),
-            dma((2, NZ - 1)), dma((2, NZ - 1)),
-            dma((NZ + 1,)), dma((NZ + 1,)),
+            dma((WAVES, NZ)), dma((WAVES, NZ)),
+            dma((WAVES, NZ - 1)), dma((WAVES, NZ - 1)),
+            dma((WAVES, 2, NZ - 1)), dma((WAVES, 2, NZ - 1)),
+            dma((WAVES,)), dma((WAVES,)),
+            dma((WAVES, NZ - 1)), dma((WAVES, NZ - 1)),
+            dma((WAVES, 2, NZ - 1)), dma((WAVES, 2, NZ - 1)),
+            dma((WAVES, NZ + 1)), dma((WAVES, NZ + 1)),
         ],
         compiler_params=pltpu.CompilerParams(
             collective_id=0, has_side_effects=True, vmem_limit_bytes=48 * 1024 * 1024

time: 109 us -> 109 us (level)
  no operation moved by 1% of the time
where the time goes in v3:
time: 109 us; the launch traced here: 108 us
  Pallas kernels  107 us (98%)
    pallas_call x1, Pallas kernels, per_device(): pl.pallas_call(functools.partial(kernel, scale), out_shape=(pltpu.VMEM((r...  106 us

profile of v3, /device:TPU:10, one launch (start us, length us, event | category | flops | bytes accessed | tf_op | source)
XLA Modules:
  0.0 107.9 jit_solution(14105719901060509269)
XLA Ops:
  0.6 105.9 %gossip_muon.1 = (bf16[2048,512]{1,0:T(8,128)(2,1)S(1)}, f32[128,512]{1,0:T(8,128)S(1)}) custom-call(f32[2048,512]{1,0:T(8,128)} %bitcast.6, bf16[2,2048,512]{2,1,0:T(8,128)(2,1)} %bitcast.7, bf16[2048,512]{1,0:T(8,128)(2,1)} %bitcast.8, f32[128,512]{1,0:T(8,128)} %bitcast.9), custom_call_target="tpu_custom_call" | custom-call | tf_op jit(solution)/shard_map/gossip_muon/pallas_call | solution.py:433
  106.5 1.4 %write_out.1 = (bf16[2048,512]{1,0:T(8,128)(2,1)}, f32[128,512]{1,0:T(8,128)}) custom-call(bf16[2048,512]{1,0:T(8,128)(2,1)S(1)} %get-tuple-element.6.w_v, f32[128,512]{1,0:T(8,128)S(1)} %get-tuple-element.7.o_v), custom_call_target="tpu_custom_call" | custom-call | tf_op jit(solution)/shard_map/write_out/pallas_call | solution.py:477

commit v4 on v3

--- a/solution.py
+++ b/solution.py
@@ -17,9 +17,13 @@
 GROUP = 256
 LAG = 4
 
-STEPS_0 = (4, 3)
-STEPS_1 = (3, 4)
+STEPS_0 = ((4, 3), (3, 4))
+STEPS_1 = ((3, 4), (4, 3))
+PIECES = 4
 WAVES = 2
+ORDER = (
+    ('first', 0), ('first', 1), ('reduce', 0, 1), ('reduce', 1, 1), ('reduce', 0, 2), ('reduce', 1, 2), ('reduce', 0, 3), ('reduce', 1, 3), ('a', 0), ('a', 1), ('b', 0), ('g0', 0, 1), ('g0', 1, 1), ('b', 1), ('c', 0), ('g0', 0, 2), ('g0', 1, 2), ('c', 1), ('g1', 0, 1), ('g1', 1, 1), ('g0', 0, 3), ('g0', 1, 3), ('g1', 0, 2), ('g1', 1, 2), ('g0', 0, 4), ('g0', 1, 4), ('g1', 0, 3), ('g1', 1, 3), ('g1', 0, 4), ('g1', 1, 4),
+)
 X_ORDER = (4, 5, 3, 6, 2, 7, 1, 0)
 
 
@@ -36,9 +40,8 @@
     m_v, g_v, w_v, o_v,
     a_in, b_in, a_out, b_out, x0, gram, d0, f_v, norm, e_v, xs, xr, r0, r1, rx,
     load_sem, small_sem,
-    a_recv, b_recv, ab_send,
-    xr_recv, xr_send, r0_recv, r0_send, r1_recv, r1_send, rx_recv, rx_send,
-    g0_recv, g0_send, g1_recv, g1_send, gx_recv, gx_send,
+    a_recv, b_recv, ab_send, send_sem,
+    xr_recv, r0_recv, r1_recv, rx_recv, g0_recv, g1_recv, gx_recv,
 ):
     rows, cols = m_v.shape
     half = cols // 2
@@ -68,17 +71,17 @@
     def span(i, n):
         return pl.ds(pl.multiple_of(i * n, n), n)
 
-    def load(i):
+    def start_load(i):
         s = span(i, GROUP)
-        return (
-            pltpu.make_async_copy(m_hbm.at[s], m_v.at[s], load_sem.at[0, i]),
-            pltpu.make_async_copy(g_hbm.at[0, s], g_v.at[0, s], load_sem.at[1, i]),
-            pltpu.make_async_copy(g_hbm.at[1, s], g_v.at[1, s], load_sem.at[2, i]),
-        )
+        pltpu.make_async_copy(m_hbm.at[s], m_v.at[s], load_sem.at[i]).start()
+        pltpu.make_async_copy(g_hbm.at[:, s], g_v.at[:, s], load_sem.at[i]).start()
+
+    def wait_load(i):
+        s = pl.ds(0, 2 * GROUP)
+        pltpu.make_async_copy(m_hbm.at[s], m_v.at[s], load_sem.at[i]).wait()
 
     for i in range(groups):
-        for c in load(i):
-            c.start()
+        start_load(i)
     own_rows = span(me, block)
     small = (
         pltpu.make_async_copy(w_hbm.at[own_rows], w_v, small_sem.at[0]),
@@ -119,8 +122,7 @@
     def _():
         @pl.loop(0, groups)
         def _(j):
-            for c in load(j):
-                c.wait()
+            wait_load(j)
             for k in range(per):
                 i = j * per + k
                 s = span(i, CHUNK)
@@ -146,8 +148,7 @@
 
         @pl.loop(0, groups)
         def _(j):
-            for c in load(j):
-                c.wait()
+            wait_load(j)
             for k in range(per):
                 i = j * per + k
                 s = span(i, CHUNK)
@@ -197,7 +198,7 @@
     def send_xr(v, k):
         zz = at_z(k)
         src = xs.at[0, v, (1 - xl) * NZ + zz]
-        return send(src, xr.at[v, zz], xr_send.at[v, k], xr_recv.at[v, k], over)
+        return send(src, xr.at[v, zz], send_sem.at[0], xr_recv.at[v, k], over)
 
     def slot(steps, way, t):
         return (0 if way > 0 else steps[0]) + t - 1
@@ -212,20 +213,20 @@
         return 1 - xl if jj == 0 else xl
 
     def send_r0(v, way, t, src):
-        i = slot(STEPS_0, way, t)
-        return send(src, r0.at[v, i], r0_send.at[v, i], r0_recv.at[v, i], towards(way))
+        i = slot(STEPS_0[v], way, t)
+        return send(src, r0.at[v, i], send_sem.at[0], r0_recv.at[v, i], towards(way))
 
     def send_r1(v, jj, way, t, src):
-        i = slot(STEPS_1, way, t)
-        return send(src, r1.at[v, jj, i], r1_send.at[v, jj, i], r1_recv.at[v, jj, i], towards(way))
+        i = slot(STEPS_1[v], way, t)
+        return send(src, r1.at[v, jj, i], send_sem.at[0], r1_recv.at[v, jj, i], towards(way))
 
     def offset(way, n, t):
         return way * (n + 1 - t)
 
-    sent = []
-
-    def go(c):
-        sent.append(c)
+    sent = [0, 0]
+
+    def go(c, phase=0):
+        sent[phase] += part // 2
         c.start()
 
     e = e_v[...]
@@ -241,7 +242,7 @@
         for v in range(WAVES):
             go(send_xr(v, k))
             for way in (1, -1):
-                n = steps_of(STEPS_1, way)
+                n = steps_of(STEPS_1[v], way)
                 if (way * n) % NZ == k:
                     for jj in range(2):
                         go(send_r1(v, jj, way, 1, xs.at[1, v, x_of(jj) * NZ + zz]))
@@ -253,21 +254,21 @@
 
     def first_0(v):
         for way in (1, -1):
-            zz, own = own_0(v, offset(way, steps_of(STEPS_0, way), 1))
+            zz, own = own_0(v, offset(way, steps_of(STEPS_0[v], way), 1))
             xr[v, zz] = own.astype(BF16)
             go(send_r0(v, way, 1, xr.at[v, zz]))
 
     def forward_0(v, way, t):
-        n = steps_of(STEPS_0, way)
-        i = slot(STEPS_0, way, t)
+        n = steps_of(STEPS_0[v], way)
+        i = slot(STEPS_0[v], way, t)
         send_r0(v, way, t, r0.at[v, i]).wait_recv()
         _, own = own_0(v, offset(way, n, t + 1))
         r0[v, i] = (r0[v, i].astype(F32) + own).astype(BF16)
         go(send_r0(v, way, t + 1, r0.at[v, i]))
 
     def forward_1(v, jj, way, t):
-        n = steps_of(STEPS_1, way)
-        i = slot(STEPS_1, way, t)
+        n = steps_of(STEPS_1[v], way)
+        i = slot(STEPS_1[v], way, t)
         send_r1(v, jj, way, t, r1.at[v, jj, i]).wait_recv()
         own = xs[1, v, x_of(jj) * NZ + at_z(offset(way, n, t + 1))]
         r1[v, jj, i] = (r1[v, jj, i].astype(F32) + own.astype(F32)).astype(BF16)
@@ -276,17 +277,17 @@
     def reduce_step(v, t):
         for jj in range(2):
             for way in (1, -1):
-                if t < steps_of(STEPS_1, way):
+                if t < steps_of(STEPS_1[v], way):
                     forward_1(v, jj, way, t)
         for way in (1, -1):
-            if t < steps_of(STEPS_0, way):
+            if t < steps_of(STEPS_0[v], way):
                 forward_0(v, way, t)
 
     def last_1(v, jj):
         out = xs[1, v, x_of(jj) * NZ + z].astype(F32)
         for way in (1, -1):
-            n = steps_of(STEPS_1, way)
-            i = slot(STEPS_1, way, n)
+            n = steps_of(STEPS_1[v], way)
+            i = slot(STEPS_1[v], way, n)
             send_r1(v, jj, way, n, r1.at[v, jj, i]).wait_recv()
             out += r1[v, jj, i].astype(F32)
         return out
@@ -294,15 +295,15 @@
     def last_0(v):
         _, out = own_0(v, 0)
         for way in (1, -1):
-            n = steps_of(STEPS_0, way)
-            i = slot(STEPS_0, way, n)
+            n = steps_of(STEPS_0[v], way)
+            i = slot(STEPS_0[v], way, n)
             send_r0(v, way, n, r0.at[v, i]).wait_recv()
             out += r0[v, i].astype(F32)
         return out
 
     def cross(v):
         src = xs.at[1, v, (1 - xl) * NZ + z]
-        return send(src, rx.at[v], rx_send.at[v], rx_recv.at[v], over)
+        return send(src, rx.at[v], send_sem.at[0], rx_recv.at[v], over)
 
     def rows_of(v, b):
         return pl.ds(pl.multiple_of(b * block + v * part, part), part)
@@ -317,36 +318,36 @@
         out_v[rows_of(v, me), c] = (w_v[r, c].astype(F32) - fresh).astype(BF16)
 
     def send_g0(v, way, t, p):
-        i = slot(STEPS_0, way, t)
-        return send(p, p, g0_send.at[v, i], g0_recv.at[v, i], towards(way))
+        i = slot(STEPS_0[v], way, t)
+        return send(p, p, send_sem.at[1], g0_recv.at[v, i], towards(way))
 
     def send_g1(v, jj, way, t, p):
-        i = slot(STEPS_1, way, t)
-        return send(p, p, g1_send.at[v, jj, i], g1_recv.at[v, jj, i], towards(way))
+        i = slot(STEPS_1[v], way, t)
+        return send(p, p, send_sem.at[1], g1_recv.at[v, jj, i], towards(way))
 
     def send_gx(v, k, p):
-        return send(p, p, gx_send.at[v, k], gx_recv.at[v, k], over)
+        return send(p, p, send_sem.at[1], gx_recv.at[v, k], over)
 
     def gather_0(v, t):
         for way in (1, -1):
-            n = steps_of(STEPS_0, way)
+            n = steps_of(STEPS_0[v], way)
             if t <= n:
                 k = (-way * t) % NZ
                 p = piece(v, side + at_z(k), 0)
                 send_g0(v, way, t, p).wait_recv()
                 if t < n:
-                    go(send_g0(v, way, t + 1, p))
-                go(send_gx(v, k, p))
+                    go(send_g0(v, way, t + 1, p), 1)
+                go(send_gx(v, k, p), 1)
 
     def gather_1(v, t):
         for jj in (1, 0):
             for way in (1, -1):
-                n = steps_of(STEPS_1, way)
+                n = steps_of(STEPS_1[v], way)
                 if t <= n:
                     p = piece(v, x_of(jj) * NZ + at_z(-way * t), 1)
                     send_g1(v, jj, way, t, p).wait_recv()
                     if t < n:
-                        go(send_g1(v, jj, way, t + 1, p))
+                        go(send_g1(v, jj, way, t + 1, p), 1)
 
     def end_a(v):
         xs[1, v, (1 - xl) * NZ + z] = last_1(v, 0).astype(BF16)
@@ -354,54 +355,38 @@
         outer(v, 0, last_0(v))
         p = piece(v, me, 0)
         for way in (1, -1):
-            go(send_g0(v, way, 1, p))
-        go(send_gx(v, 0, p))
+            go(send_g0(v, way, 1, p), 1)
+        go(send_gx(v, 0, p), 1)
 
     def end_b(v):
         total_1 = last_1(v, 1)
         cross(v).wait_recv()
         outer(v, 1, total_1 + rx[v].astype(F32))
         p = piece(v, me, 1)
-        go(send_gx(v, NZ, p))
-        for way in (1, -1):
-            go(send_g1(v, 1, way, 1, p))
+        go(send_gx(v, NZ, p), 1)
+        for way in (1, -1):
+            go(send_g1(v, 1, way, 1, p), 1)
 
     def end_c(v):
         p = piece(v, over, 1)
         send_gx(v, NZ, p).wait_recv()
         for way in (1, -1):
-            go(send_g1(v, 0, way, 1, p))
-
-    def both(step, *args):
-        for v in range(WAVES):
-            step(v, *args)
-
-    both(first_0)
-    for t in range(1, 4):
-        both(reduce_step, t)
+            go(send_g1(v, 0, way, 1, p), 1)
+
+    steps = dict(
+        first=first_0, reduce=reduce_step, a=end_a, b=end_b, c=end_c, g0=gather_0, g1=gather_1
+    )
     for c in small:
         c.wait()
-    both(end_a)
-    end_b(0)
-    both(gather_0, 1)
-    for v in range(1, WAVES):
-        end_b(v)
-    end_c(0)
-    both(gather_0, 2)
-    for v in range(1, WAVES):
-        end_c(v)
-    both(gather_1, 1)
-    both(gather_0, 3)
-    both(gather_1, 2)
-    both(gather_0, 4)
-    both(gather_1, 3)
-    both(gather_1, 4)
+    for step, *args in ORDER:
+        steps[step](*args)
     for v in range(WAVES):
         for k in range(NZ):
             send_gx(v, k, piece(v, (1 - xl) * NZ + at_z(k), 0)).wait_recv()
 
-    for c in sent:
-        c.wait_send()
+    for phase in range(2):
+        r = pl.ds(0, sent[phase])
+        send(a_out.at[r], a_in.at[r], send_sem.at[phase], a_recv.at[0], pair).wait_send()
     send(a_out, a_in, ab_send.at[0], a_recv.at[0], pair).wait_send()
 
     @pl.when(jnp.logical_not(edge))
@@ -410,10 +395,11 @@
 
 
 def write_out(w_v, o_v, w_hbm, o_hbm, sem):
-    copies = (
-        pltpu.make_async_copy(w_v, w_hbm, sem.at[0]),
-        pltpu.make_async_copy(o_v, o_hbm, sem.at[1]),
-    )
+    n = w_v.shape[0] // PIECES
+    copies = [pltpu.make_async_copy(o_v, o_hbm, sem.at[PIECES])]
+    for i in range(PIECES):
+        s = pl.ds(i * n, n)
+        copies.append(pltpu.make_async_copy(w_v.at[s], w_hbm.at[s], sem.at[i]))
     for c in copies:
         c.start()
     for c in copies:
@@ -455,16 +441,17 @@
             pltpu.VMEM((WAVES, NZ - 1, part, half), BF16),
             pltpu.VMEM((WAVES, 2, NZ - 1, part, half), BF16),
             pltpu.VMEM((WAVES, part, half), BF16),
-            dma((3, groups)),
+            dma((groups,)),
             dma((2,)),
             dma((chunks,)), dma((chunks,)), dma((2,)),
-            dma((WAVES, NZ)), dma((WAVES, NZ)),
-            dma((WAVES, NZ - 1)), dma((WAVES, NZ - 1)),
-            dma((WAVES, 2, NZ - 1)), dma((WAVES, 2, NZ - 1)),
-            dma((WAVES,)), dma((WAVES,)),
-            dma((WAVES, NZ - 1)), dma((WAVES, NZ - 1)),
-            dma((WAVES, 2, NZ - 1)), dma((WAVES, 2, NZ - 1)),
-            dma((WAVES, NZ + 1)), dma((WAVES, NZ + 1)),
+            dma((2,)),
+            dma((WAVES, NZ)),
+            dma((WAVES, NZ - 1)),
+            dma((WAVES, 2, NZ - 1)),
+            dma((WAVES,)),
+            dma((WAVES, NZ - 1)),
+            dma((WAVES, 2, NZ - 1)),
+            dma((WAVES, NZ + 1)),
         ],
         compiler_params=pltpu.CompilerParams(
             collective_id=0, has_side_effects=True, vmem_limit_bytes=48 * 1024 * 1024
@@ -482,7 +469,7 @@
         ),
         in_specs=[vmem_spec] * 2,
         out_specs=(any_spec, any_spec),
-        scratch_shapes=[dma((2,))],
+        scratch_shapes=[dma((PIECES + 1,))],
         name="write_out",
     )(
         pltpu.with_memory_space_constraint(new_weights, pltpu.VMEM),

time: 109 us -> 109 us (level)
  no operation moved by 1% of the time
where the time goes in v4:
time: 109 us; the launch traced here: 108 us
  Pallas kernels  107 us (98%)
    pallas_call x1, Pallas kernels, per_device(): pl.pallas_call(functools.partial(kernel, scale), out_shape=(pltpu.VMEM((r...  106 us

profile of v4, /device:TPU:10, one launch (start us, length us, event | category | flops | bytes accessed | tf_op | source)
XLA Modules:
  0.0 107.6 jit_solution(9687222381290615199)
XLA Ops:
  0.6 105.5 %gossip_muon.1 = (bf16[2048,512]{1,0:T(8,128)(2,1)S(1)}, f32[128,512]{1,0:T(8,128)S(1)}) custom-call(f32[2048,512]{1,0:T(8,128)} %bitcast.6, bf16[2,2048,512]{2,1,0:T(8,128)(2,1)} %bitcast.7, bf16[2048,512]{1,0:T(8,128)(2,1)} %bitcast.8, f32[128,512]{1,0:T(8,128)} %bitcast.9), custom_call_target="tpu_custom_call" | custom-call | tf_op jit(solution)/shard_map/gossip_muon/pallas_call | solution.py:419
  106.2 1.4 %write_out.1 = (bf16[2048,512]{1,0:T(8,128)(2,1)}, f32[128,512]{1,0:T(8,128)}) custom-call(bf16[2048,512]{1,0:T(8,128)(2,1)S(1)} %get-tuple-element.6.w_v, f32[128,512]{1,0:T(8,128)S(1)} %get-tuple-element.7.o_v), custom_call_target="tpu_custom_call" | custom-call | tf_op jit(solution)/shard_map/write_out/pallas_call | solution.py:464

commit v5 on v4

--- a/solution.py
+++ b/solution.py
@@ -14,11 +14,11 @@
 F32, BF16 = jnp.float32, jnp.bfloat16
 
 CHUNK = 32
-GROUP = 256
+GROUP = 128
 LAG = 4
 
-STEPS_0 = ((4, 3), (3, 4))
-STEPS_1 = ((3, 4), (4, 3))
+STEPS_0 = ((4, 3), (4, 3))
+STEPS_1 = ((3, 4), (3, 4))
 PIECES = 4
 WAVES = 2
 ORDER = (
@@ -326,7 +326,7 @@
         return send(p, p, send_sem.at[1], g1_recv.at[v, jj, i], towards(way))
 
     def send_gx(v, k, p):
-        return send(p, p, send_sem.at[1], gx_recv.at[v, k], over)
+        return send(p, p, send_sem.at[1], gx_recv.at[v, k // NZ], over)
 
     def gather_0(v, t):
         for way in (1, -1):
@@ -381,8 +381,8 @@
     for step, *args in ORDER:
         steps[step](*args)
     for v in range(WAVES):
-        for k in range(NZ):
-            send_gx(v, k, piece(v, (1 - xl) * NZ + at_z(k), 0)).wait_recv()
+        r = pl.ds(0, NZ * part // 2)
+        send(a_out.at[r], a_in.at[r], send_sem.at[1], gx_recv.at[v, 0], over).wait_recv()
 
     for phase in range(2):
         r = pl.ds(0, sent[phase])
@@ -451,7 +451,7 @@
             dma((WAVES,)),
             dma((WAVES, NZ - 1)),
             dma((WAVES, 2, NZ - 1)),
-            dma((WAVES, NZ + 1)),
+            dma((WAVES, 2)),
         ],
         compiler_params=pltpu.CompilerParams(
             collective_id=0, has_side_effects=True, vmem_limit_bytes=48 * 1024 * 1024

time: 109 us -> 107 us (0.982); the launches traced: 108 us -> 107 us
  no operation moved by 1% of the time
where the time goes in v5:
time: 107 us
  Pallas kernels  107 us (100%)
    pallas_call x1, Pallas kernels, per_device(): pl.pallas_call(functools.partial(kernel, scale), out_shape=(pltpu.VMEM((r...  105 us

profile of v5, /device:TPU:10, one launch (start us, length us, event | category | flops | bytes accessed | tf_op | source)
XLA Modules:
  0.0 107.2 jit_solution(13583872262512296739)
XLA Ops:
  0.6 105.1 %gossip_muon.1 = (bf16[2048,512]{1,0:T(8,128)(2,1)S(1)}, f32[128,512]{1,0:T(8,128)S(1)}) custom-call(f32[2048,512]{1,0:T(8,128)} %bitcast.6, bf16[2,2048,512]{2,1,0:T(8,128)(2,1)} %bitcast.7, bf16[2048,512]{1,0:T(8,128)(2,1)} %bitcast.8, f32[128,512]{1,0:T(8,128)} %bitcast.9), custom_call_target="tpu_custom_call" | custom-call | tf_op jit(solution)/shard_map/gossip_muon/pallas_call | solution.py:419
  105.8 1.4 %write_out.1 = (bf16[2048,512]{1,0:T(8,128)(2,1)}, f32[128,512]{1,0:T(8,128)}) custom-call(bf16[2048,512]{1,0:T(8,128)(2,1)S(1)} %get-tuple-element.6.w_v, f32[128,512]{1,0:T(8,128)S(1)} %get-tuple-element.7.o_v), custom_call_target="tpu_custom_call" | custom-call | tf_op jit(solution)/shard_map/write_out/pallas_call | solution.py:464

commit v6 on v5

--- a/solution.py
+++ b/solution.py
@@ -19,7 +19,7 @@
 
 STEPS_0 = ((4, 3), (4, 3))
 STEPS_1 = ((3, 4), (3, 4))
-PIECES = 4
+PIECES = 1
 WAVES = 2
 ORDER = (
     ('first', 0), ('first', 1), ('reduce', 0, 1), ('reduce', 1, 1), ('reduce', 0, 2), ('reduce', 1, 2), ('reduce', 0, 3), ('reduce', 1, 3), ('a', 0), ('a', 1), ('b', 0), ('g0', 0, 1), ('g0', 1, 1), ('b', 1), ('c', 0), ('g0', 0, 2), ('g0', 1, 2), ('c', 1), ('g1', 0, 1), ('g1', 1, 1), ('g0', 0, 3), ('g0', 1, 3), ('g1', 0, 2), ('g1', 1, 2), ('g0', 0, 4), ('g0', 1, 4), ('g1', 0, 3), ('g1', 1, 3), ('g1', 0, 4), ('g1', 1, 4),
@@ -218,7 +218,11 @@
 
     def send_r1(v, jj, way, t, src):
         i = slot(STEPS_1[v], way, t)
-        return send(src, r1.at[v, jj, i], send_sem.at[0], r1_recv.at[v, jj, i], towards(way))
+        return send(src, r1.at[v, jj, i], send_sem.at[0], r1_recv.at[v, i], towards(way))
+
+    def wait_r1(v, i):
+        r = pl.ds(0, part)
+        send(a_out.at[r], a_in.at[r], send_sem.at[0], r1_recv.at[v, i], pair).wait_recv()
 
     def offset(way, n, t):
         return way * (n + 1 - t)
@@ -269,7 +273,8 @@
     def forward_1(v, jj, way, t):
         n = steps_of(STEPS_1[v], way)
         i = slot(STEPS_1[v], way, t)
-        send_r1(v, jj, way, t, r1.at[v, jj, i]).wait_recv()
+        if jj == 0:
+            wait_r1(v, i)
         own = xs[1, v, x_of(jj) * NZ + at_z(offset(way, n, t + 1))]
         r1[v, jj, i] = (r1[v, jj, i].astype(F32) + own.astype(F32)).astype(BF16)
         go(send_r1(v, jj, way, t + 1, r1.at[v, jj, i]))
@@ -288,7 +293,8 @@
         for way in (1, -1):
             n = steps_of(STEPS_1[v], way)
             i = slot(STEPS_1[v], way, n)
-            send_r1(v, jj, way, n, r1.at[v, jj, i]).wait_recv()
+            if jj == 0:
+                wait_r1(v, i)
             out += r1[v, jj, i].astype(F32)
         return out
 
@@ -447,7 +453,7 @@
             dma((2,)),
             dma((WAVES, NZ)),
             dma((WAVES, NZ - 1)),
-            dma((WAVES, 2, NZ - 1)),
+            dma((WAVES, NZ - 1)),
             dma((WAVES,)),
             dma((WAVES, NZ - 1)),
             dma((WAVES, 2, NZ - 1)),

time: 107 us -> 108 us (level)
  no operation moved by 1% of the time
where the time goes in v6:
time: 108 us; the launch traced here: 107 us
  Pallas kernels  107 us (99%)
    pallas_call x1, Pallas kernels, per_device(): pl.pallas_call(functools.partial(kernel, scale), out_shape=(pltpu.VMEM((r...  105 us

profile of v6, /device:TPU:10, one launch (start us, length us, event | category | flops | bytes accessed | tf_op | source)
XLA Modules:
  0.0 107.3 jit_solution(656119140268350978)
XLA Ops:
  0.6 105.2 %gossip_muon.1 = (bf16[2048,512]{1,0:T(8,128)(2,1)S(1)}, f32[128,512]{1,0:T(8,128)S(1)}) custom-call(f32[2048,512]{1,0:T(8,128)} %bitcast.6, bf16[2,2048,512]{2,1,0:T(8,128)(2,1)} %bitcast.7, bf16[2048,512]{1,0:T(8,128)(2,1)} %bitcast.8, f32[128,512]{1,0:T(8,128)} %bitcast.9), custom_call_target="tpu_custom_call" | custom-call | tf_op jit(solution)/shard_map/gossip_muon/pallas_call | solution.py:425
  105.9 1.4 %write_out.1 = (bf16[2048,512]{1,0:T(8,128)(2,1)}, f32[128,512]{1,0:T(8,128)}) custom-call(bf16[2048,512]{1,0:T(8,128)(2,1)S(1)} %get-tuple-element.6.w_v, f32[128,512]{1,0:T(8,128)S(1)} %get-tuple-element.7.o_v), custom_call_target="tpu_custom_call" | custom-call | tf_op jit(solution)/shard_map/write_out/pallas_call | solution.py:470
